TPU v7x, 32 devices: a whole 2x2x4 slice. The times are simulated.
32 devices in a mesh: rep: 4 (over z), inst: 8 (over y, x, core).
Axes of the slice: x: 2, y: 2, z: 4, core: 2. Of those that a mesh axis runs over, the one named last changes fastest.
Arguments:
- acts: bfloat16 [32768, 4096], P(('rep', 'inst')), may hold values from -6 to 6
- grad_keys: bfloat16 [32768, 1024], P(('rep', 'inst')), may hold values from -0.0625 to 0.0625
- grad_values: bfloat16 [32768, 1024], P(('rep', 'inst')), may hold values from -0.0625 to 0.0625
- grad_logits: bfloat16 [8, 32768], P(None, ('rep', 'inst')), may hold values from -0.0625 to 0.0625
- order: int32 [32], replicated, may hold values from 0 to 31, each once
- bucket_param: float32 [4, 2048, 1024], P(None, 'inst'), may hold values from -6 to 6
- bucket_m: float32 [4, 2048, 1024], P(None, 'inst'), may hold values from -6 to 6
- bucket_v: float32 [4, 2048, 1024], P(None, 'inst'), may hold values from 0.25 to 4
- router_param: float32 [32, 1024], P('inst'), may hold values from -6 to 6
- router_m: float32 [32, 1024], P('inst'), may hold values from -6 to 6
- router_v: float32 [32, 1024], P('inst'), may hold values from 0.25 to 4
Outputs:
- new_param: float32 [4, 2048, 1024], P(None, 'inst')
- new_moment: float32 [4, 2048, 1024], P(None, 'inst')
- new_second: float32 [4, 2048, 1024], P(None, 'inst')
- router_new_param: float32 [32, 1024], P('inst')
- router_new_moment: float32 [32, 1024], P('inst')
- router_new_second: float32 [32, 1024], P('inst')
Inputs may be any that keep to these rules, and one draw needn't show every extreme that they name: order is a permutation of the 32 row blocks; entries with k * 8 <= s < (k + 1) * 8 fill bucket k.
All inputs are finite; a program needn't handle non-finite values.
Results may differ from a plain program's by a relative error of at most 0.0003.
Values sent between devices are 32-bit elements; how exact they have to be, the bound alone decides.
A program may use at most 256 MiB of HBM per device.

v0:
```python
import functools

import jax
import jax.numpy as jnp
from jax import lax
from jax.experimental import pallas as pl
from jax.experimental.pallas import tpu as pltpu
from jax.sharding import PartitionSpec as P

MESH = pl.DeviceIdType.MESH
BUCKETS = 4
BLOCK_ROWS = 256
COLS = 128
LAG = 1
SPLIT = 2
RING = 4
VMEM_BYTES = 42 * 2**20


beta_first = 0.9
beta_second = 0.95
step_rate = 0.05
decay_rate = 0.1
epsilon = 1e-08
correct_first = 1.0 - 0.9**10
correct_second = 1.0 - 0.95**10


def adamw(grad, param, moment, second):
    moment_new = beta_first * moment + (1.0 - beta_first) * grad
    second_new = beta_second * second + (1.0 - beta_second) * grad * grad
    ratio = moment_new / correct_first / (jnp.sqrt(second_new / correct_second) + epsilon)
    param_new = param - step_rate * (ratio + decay_rate * param)
    return (param_new, moment_new, second_new)


def when_between(p, count, body):
    @pl.when(jnp.logical_and(p >= 0, p < count))
    def _():
        body(p)


class Lane:
    def __init__(self, n_inst, n_rep, dims, parts, send, recv, halves, lefts, rights, finish):
        self.n_inst, self.n_rep, self.dims = n_inst, n_rep, dims
        self.parts, self.send, self.recv = parts, send, recv
        self.halves, self.lefts, self.rights, self.finish = halves, lefts, rights, finish
        self.me = lax.axis_index("inst")
        self.rep = lax.axis_index("rep")
        self.stages = len(dims)
        self.base = 1 + LAG * (self.stages - 1)
        self.left = n_rep // 2 - 1
        self.top = self.base + LAG * (self.left + 1)

    def partner(self, bit):
        return self.me + (1 - 2 * ((self.me // 2**bit) % 2)) * 2**bit

    def owner(self, q):
        index = self.me
        for at, bit in enumerate(self.dims):
            if (q >> (self.stages - 1 - at)) & 1:
                index = index + (1 - 2 * ((self.me // 2**bit) % 2)) * 2**bit
        return index

    def copy(self, src, dst, stage, p, **device):
        return pltpu.make_async_remote_copy(
            src_ref=src,
            dst_ref=dst,
            send_sem=self.send.at[stage, p],
            recv_sem=self.recv.at[stage, p],
            device_id=device,
            device_id_type=MESH,
        )

    def half_copy(self, stage, p):
        count = self.n_inst >> (stage + 1)
        source = self.parts(p) if stage == 0 else self.halves(stage - 1, p)
        return self.copy(
            source.at[pl.ds(count, count)],
            self.halves(stage, p),
            stage,
            p,
            inst=self.partner(self.dims[stage]),
        )

    def add_half(self, stage, p):
        self.half_copy(stage, p).wait()
        count = self.n_inst >> (stage + 1)
        source = self.parts(p) if stage == 0 else self.halves(stage - 1, p)
        into = self.halves(stage, p)
        into[...] += source[pl.ds(0, count)]

    def total(self, p):
        return self.halves(self.stages - 1, p)

    def to_right(self, src, p):
        return self.copy(src, self.lefts(p), self.stages, p, rep=self.rep + 1)

    def to_left(self, src, p):
        return self.copy(src, self.rights(p), self.stages + 1, p, rep=self.rep - 1)

    def reduce_ends(self, p):
        if self.left > 0:

            @pl.when(self.rep == 0)
            def _():
                self.to_right(self.total(p), p).start()

            @pl.when(self.rep == self.n_rep - 1)
            def _():
                self.to_left(self.total(p), p).start()

    def from_left(self, p):
        self.to_right(self.total(p), p).wait_recv()

    def from_right(self, p):
        self.to_left(self.total(p), p).wait_recv()

    def reduce(self, t, count):
        rep, last = self.rep, self.n_rep - 1

        def towards_right(p):
            total = self.total(p)
            if self.left > 0:
                self.from_left(p)
                total[...] += self.lefts(p)[...]
            self.to_right(total, p).start()

        def towards_left(p):
            total = self.total(p)
            if self.left > 0:
                self.from_right(p)
                total[...] += self.rights(p)[...]
            self.to_left(total, p).start()

        first = min(1, self.left)
        p = t - self.base - LAG * rep

        @pl.when((rep >= first) & (rep <= self.left) & (p >= 0) & (p < count))
        def _():
            towards_right(p)

        p2 = t - self.base - LAG * (last - rep)

        @pl.when((rep > self.left) & (rep <= last - first) & (p2 >= 0) & (p2 < count))
        def _():
            towards_left(p2)

    def spread(self, t, count):
        rep, left, last = self.rep, self.left, self.n_rep - 1
        p = t - self.top - LAG * (left - rep)

        @pl.when((rep <= left) & (p >= 0) & (p < count))
        def _():
            self.from_right(p)
            whole = self.rights(p)

            @pl.when(rep == left)
            def _():
                whole[...] += self.total(p)[...]

            if left > 0:

                @pl.when(rep > 0)
                def _():
                    self.to_left(whole, p).start()

            self.finish(whole, p)

        p2 = t - self.top - LAG * (rep - left - 1)

        @pl.when((rep > left) & (p2 >= 0) & (p2 < count))
        def _():
            self.from_left(p2)
            whole = self.lefts(p2)

            @pl.when(rep == left + 1)
            def _():
                whole[...] += self.total(p2)[...]

            if left > 0:

                @pl.when(rep < last)
                def _():
                    self.to_right(whole, p2).start()

            self.finish(whole, p2)

    def settle(self, p):
        @pl.when(self.rep < self.n_rep - 1)
        def _():
            self.to_right(self.total(p), p).wait_send()

        @pl.when(self.rep > 0)
        def _():
            self.to_left(self.total(p), p).wait_send()

    def last_step(self):
        return self.top + LAG * self.left


def kernel(
    n_inst,
    n_rep,
    order,
    acts,
    keys_in,
    values_in,
    logits_in,
    out,
    router_out,
    slabs,
    keys,
    values,
    logits,
    turned,
    router_all,
    parts,
    router_parts,
    load,
    *scratch,
):
    bits = n_inst.bit_length() - 1
    rows = slabs.shape[-1]
    short = parts.shape[-1]
    width = router_parts.shape[-1]
    per_bucket = order.shape[0] // BUCKETS
    column_blocks = acts.shape[1] // BLOCK_ROWS
    chunks = keys.shape[1] // COLS
    split = rows // parts.shape[-1]
    count = chunks * split * BUCKETS // 2
    halves = scratch[:bits]
    ring = halves[0].shape[1]
    router_halves = scratch[bits : 2 * bits]
    lefts, rights, router_lefts, router_rights = scratch[2 * bits : 2 * bits + 4]
    sends, recvs, router_sends, router_recvs, credit = scratch[2 * bits + 4 :]

    def finish(kind):
        def body(ref, p):
            chunk = p // split
            bucket = 2 * (chunk // chunks) + kind
            start = pl.multiple_of((chunk % chunks) * COLS, COLS)
            top = pl.multiple_of((p % split) * short, short)
            out[bucket, pl.ds(top, short), pl.ds(start, COLS)] = ref[0].T

        return body

    def router_finish(ref, p):
        line = router_out.shape[1]
        for at in range(router_out.shape[0]):
            router_out[pl.ds(at, 1), :] = ref[0, :, pl.ds(at * line, line)]

    forward = [0] + list(range(1, bits))
    backward = [0] + list(range(bits - 1, 0, -1))
    lanes = []
    for kind, dims in enumerate((forward, backward)):
        lanes.append(
            Lane(
                n_inst,
                n_rep,
                dims,
                lambda p, kind=kind: parts.at[kind, p % (2 * split)],
                sends.at[kind],
                recvs.at[kind],
                lambda stage, p, kind=kind: halves[stage].at[kind, p if stage else p % ring],
                lambda p, kind=kind: lefts.at[kind, p],
                lambda p, kind=kind: rights.at[kind, p],
                finish(kind),
            )
        )
    router = Lane(
        n_inst,
        n_rep,
        forward,
        lambda p: router_parts,
        router_sends,
        router_recvs,
        lambda stage, p: router_halves[stage],
        lambda p: router_lefts,
        lambda p: router_rights,
        router_finish,
    )
    me, rep = lax.axis_index("inst"), lax.axis_index("rep")

    loads = [
        pltpu.make_async_copy(acts.at[:, pl.ds(at * rows, rows)], slabs.at[at], load.at[at])
        for at in range(slabs.shape[0])
    ]
    ends = ((keys_in, keys), (values_in, values), (logits_in, logits))
    loads += [
        pltpu.make_async_copy(src, dst, load.at[slabs.shape[0] + at])
        for at, (src, dst) in enumerate(ends)
    ]
    for copy in reversed(loads):
        copy.start()

    barrier = pltpu.get_barrier_semaphore()
    for bit in range(bits):
        pl.semaphore_signal(
            barrier, inc=1, device_id={"inst": router.partner(bit)}, device_id_type=MESH
        )

    @pl.when(rep > 0)
    def _():
        pl.semaphore_signal(barrier, inc=1, device_id={"rep": rep - 1}, device_id_type=MESH)

    @pl.when(rep < n_rep - 1)
    def _():
        pl.semaphore_signal(barrier, inc=1, device_id={"rep": rep + 1}, device_id_type=MESH)

    peers = bits + jnp.where(rep > 0, 1, 0) + jnp.where(rep < n_rep - 1, 1, 0)
    pl.semaphore_wait(barrier, peers)
    for copy in loads:
        copy.wait()

    def products(chunk):
        start = pl.multiple_of((chunk % chunks) * COLS, COLS)
        turned[0] = keys[:, pl.ds(start, COLS)].T
        turned[1] = values[:, pl.ds(start, COLS)].T
        for kind, lane in enumerate(lanes):
            bucket = 2 * (chunk // chunks) + kind
            for q in reversed(range(n_inst)):
                first = lane.owner(q) * rows
                block = order[bucket * per_bucket + first // BLOCK_ROWS]
                at = lax.rem(block, column_blocks) * (BLOCK_ROWS // rows) + first % BLOCK_ROWS // rows
                full = jnp.dot(
                    turned[lax.div(block, column_blocks)],
                    slabs[at],
                    preferred_element_type=jnp.float32,
                )
                for part in range(split):
                    slot = (chunk % 2) * split + part
                    parts[kind, slot, q] = full[:, part * short : (part + 1) * short]
            for part in range(split):
                p = chunk * split + part

                @pl.when(p >= ring)
                def _(kind=kind):
                    pl.semaphore_wait(credit.at[kind], 1)

                lane.half_copy(0, p).start()

    def router_products(p):
        for at in range(slabs.shape[0]):
            router_all[:, pl.ds(at * rows, rows)] = jnp.dot(
                logits[...], slabs[at], preferred_element_type=jnp.float32
            )
        for q in range(n_inst):
            first = router.owner(q) * width
            router_parts[q] = router_all[
                pl.ds(first // acts.shape[1], 1),
                pl.ds(pl.multiple_of(first % acts.shape[1], width), width),
            ]
        router.half_copy(0, 0).start()

    both = [(lane, count) for lane in lanes] + [(router, 1)]

    def step(t, carry):
        @pl.when((t % split == 0) & (t < count))
        def _():
            products(t // split)

        when_between(t, 1, router_products)
        for stage in range(bits):
            lag = 1 + LAG * stage
            for lane, most in both:

                def body(p, lane=lane, stage=stage):
                    lane.add_half(stage, p)
                    if stage == 1 and lane is not router:

                        @pl.when(p < count - ring)
                        def _():
                            pl.semaphore_signal(
                                credit.at[lanes.index(lane)],
                                inc=1,
                                device_id={"inst": lane.partner(0)},
                                device_id_type=MESH,
                            )

                    if stage < bits - 1:
                        lane.half_copy(stage + 1, p).start()
                    else:
                        lane.reduce_ends(p)

                when_between(t - lag, most, body)
        for lane, most in both:
            lane.reduce(t, most)
            lane.spread(t, most)
        return carry

    steps = count + max(lane.last_step() for lane, _ in both)
    lax.fori_loop(0, steps, step, 0)

    def close(p, carry):
        for lane in lanes:
            lane.settle(p)
        return carry

    lax.fori_loop(0, count, close, 0)
    router.settle(0)


def summed(order, acts, keys, values, logits, n_inst, n_rep, bucket_rows, router_size):
    bits = n_inst.bit_length() - 1
    rows = bucket_rows // n_inst
    width = router_size // n_inst
    kv = keys.shape[1]
    split = max(1, min(SPLIT, rows // 128))
    short = rows // split
    count = kv // COLS * split * BUCKETS // 2
    vmem = pl.BlockSpec(memory_space=pltpu.VMEM)
    f32 = jnp.float32
    scratch = [
        pltpu.VMEM((acts.shape[1] // rows, acts.shape[0], rows), acts.dtype),
        pltpu.VMEM(keys.shape, keys.dtype),
        pltpu.VMEM(values.shape, values.dtype),
        pltpu.VMEM(logits.shape, logits.dtype),
        pltpu.VMEM((2, COLS, acts.shape[0]), acts.dtype),
        pltpu.VMEM((logits.shape[0], acts.shape[1]), f32),
        pltpu.VMEM((2, 2 * split, n_inst, COLS, short), f32),
        pltpu.VMEM((n_inst, 1, width), f32),
        pltpu.SemaphoreType.DMA((acts.shape[1] // rows + 3,)),
    ]
    ring = min(count, RING * split)
    scratch += [
        pltpu.VMEM((2, count if s else ring, n_inst >> (s + 1), COLS, short), f32)
        for s in range(bits)
    ]
    scratch += [pltpu.VMEM((n_inst >> (s + 1), 1, width), f32) for s in range(bits)]
    scratch += [pltpu.VMEM((2, count, 1, COLS, short), f32)] * 2
    scratch += [pltpu.VMEM((1, 1, width), f32)] * 2
    scratch += [pltpu.SemaphoreType.DMA((2, bits + 2, count))] * 2
    scratch += [pltpu.SemaphoreType.DMA((bits + 2, 1))] * 2
    scratch += [pltpu.SemaphoreType.REGULAR((2,))]
    return pl.pallas_call(
        functools.partial(kernel, n_inst, n_rep),
        out_shape=(
            jax.ShapeDtypeStruct((BUCKETS, rows, kv), f32),
            jax.ShapeDtypeStruct((width // kv, kv), f32),
        ),
        in_specs=[
            pl.BlockSpec(memory_space=pltpu.SMEM),
        ]
        + [pl.BlockSpec(memory_space=pltpu.HBM)] * 4,
        out_specs=(vmem, vmem),
        scratch_shapes=scratch,
        compiler_params=pltpu.CompilerParams(
            collective_id=0, has_side_effects=True, vmem_limit_bytes=VMEM_BYTES
        ),
        cost_estimate=pl.CostEstimate(
            flops=4 * acts.shape[0] * acts.shape[1] * kv,
            bytes_accessed=16 * 2**20,
            transcendentals=0,
        ),
    )(order, acts, keys, values, logits)


def on_device(
    n_inst,
    n_rep,
    acts,
    grad_keys,
    grad_values,
    grad_logits,
    order,
    bucket_param,
    bucket_m,
    bucket_v,
    router_param,
    router_m,
    router_v,
):
    total, router_total = summed(
        order,
        acts,
        grad_keys,
        grad_values,
        grad_logits,
        n_inst,
        n_rep,
        bucket_param.shape[1] * n_inst,
        router_param.size * n_inst,
    )
    fresh = adamw(total, bucket_param, bucket_m, bucket_v)
    router_fresh = adamw(router_total.reshape(router_param.shape), router_param, router_m, router_v)
    return fresh + router_fresh


def solution(mesh):
    return jax.shard_map(
        functools.partial(on_device, mesh.shape["inst"], mesh.shape["rep"]),
        mesh=mesh,
        in_specs=(
            P(("rep", "inst"), None),
            P(("rep", "inst"), None),
            P(("rep", "inst"), None),
            P(None, ("rep", "inst")),
            P(),
            P(None, "inst", None),
            P(None, "inst", None),
            P(None, "inst", None),
            P("inst", None),
            P("inst", None),
            P("inst", None),
        ),
        out_specs=(
            P(None, "inst", None),
            P(None, "inst", None),
            P(None, "inst", None),
            P("inst", None),
            P("inst", None),
            P("inst", None),
        ),
        check_vma=False,
    )
```

profile of v0, /device:TPU:0, one launch (start us, length us, event | category | flops | bytes accessed | tf_op | source)
XLA Modules:
  0.0 185.3 jit_solution(15091333932903650225)
XLA Ops:
  0.6 0.0 copy-start
  0.6 1.6 copy-done
  2.2 0.0 copy-start.1
  2.2 1.6 copy-done.1
  3.8 0.0 copy-start.2
  3.8 0.7 copy-done.2
  4.5 0.0 copy-start.3
  4.5 0.7 copy-done.3
  5.2 0.0 copy-start.4
  5.2 0.0 copy-start.5
  5.2 0.0 copy-start.6
  5.2 173.5 %shard_map.154 = (f32[4,256,1024]{2,1,0:T(8,128)S(1)}, f32[4,1024]{1,0:T(4,128)S(1)}) custom-call(s32[32]{0:T(128)S(1)} %copy-done.3, bf16[1024,4096]{1,0:T(8,128)(2,1)} %acts.1, bf16[1024,1024]{1,0:T(8,128)(2,1)S(1)} %copy-done, bf16[1024,1024]{1,0:T(8,128)(2,1)S(1)} %copy-done.1, bf16[8,1024]{1,0:T(8,128)(2,1)S(1)} %copy-done.2), custom_call_target="tpu_custom_call" | custom-call | flops 17179869184 | bytes 16777216 | tf_op jit(solution)/shard_map/pallas_call | solution.py:436
  178.7 0.0 copy-done.4
  178.7 0.0 copy-done.5
  178.8 0.0 copy-done.6
  178.8 0.0 copy-start.7
  178.8 0.0 copy-start.8
  178.8 0.0 copy-start.9
  178.8 5.9 %multiply_subtract_fusion = (f32[4,256,1024]{2,1,0:T(8,128)}, f32[4,256,1024]{2,1,0:T(8,128)}, f32[4,256,1024]{2,1,0:T(8,128)}) fusion(f32[4,256,1024]{2,1,0:T(8,128)S(1)} %copy-done.4, f32[4,256,1024]{2,1,0:T(8,128)S(1)} %get-tuple-element.8, f32[4,256,1024]{2,1,0:T(8,128)S(1)} %copy-done.5, f32[4,256,1024]{2,1,0:T(8,128)S(1)} %copy-done.6), kind=kLoop, calls=%fused_computation.2 | loop fusion | flops 15728640 | bytes 29360128 | tf_op jit(solution)/shard_map/sub | solution.py:33
  184.7 0.0 copy-done.7
  184.7 0.0 copy-done.8
  184.7 0.0 copy-done.9
  184.7 0.6 multiply_subtract_fusion.1
Async XLA Ops:
  0.6 1.6 copy-start
  2.2 1.6 copy-start.1
  3.8 0.7 copy-start.2
  4.5 0.7 copy-start.3
  5.2 173.5 %copy-start.4 = (f32[4,256,1024]{2,1,0:T(8,128)S(1)}, f32[4,256,1024]{2,1,0:T(8,128)}, u32[]{:S(2)}) copy-start(f32[4,256,1024]{2,1,0:T(8,128)} %param.16) | copy-start | bytes 12582916
  5.2 173.6 %copy-start.5 = (f32[4,256,1024]{2,1,0:T(8,128)S(1)}, f32[4,256,1024]{2,1,0:T(8,128)}, u32[]{:S(2)}) copy-start(f32[4,256,1024]{2,1,0:T(8,128)} %param.17) | copy-start | bytes 12582916
  5.2 173.6 %copy-start.6 = (f32[4,256,1024]{2,1,0:T(8,128)S(1)}, f32[4,256,1024]{2,1,0:T(8,128)}, u32[]{:S(2)}) copy-start(f32[4,256,1024]{2,1,0:T(8,128)} %param.18) | copy-start | bytes 12582916
  178.8 5.9 %copy-start.7 = (f32[4,1024]{1,0:T(4,128)S(1)}, f32[4,1024]{1,0:T(4,128)}, u32[]{:S(2)}) copy-start(f32[4,1024]{1,0:T(4,128)} %param.19) | copy-start | bytes 49156
  178.8 5.9 %copy-start.8 = (f32[4,1024]{1,0:T(4,128)S(1)}, f32[4,1024]{1,0:T(4,128)}, u32[]{:S(2)}) copy-start(f32[4,1024]{1,0:T(4,128)} %param.20) | copy-start | bytes 49156
  178.8 5.9 %copy-start.9 = (f32[4,1024]{1,0:T(4,128)S(1)}, f32[4,1024]{1,0:T(4,128)}, u32[]{:S(2)}) copy-start(f32[4,1024]{1,0:T(4,128)} %param.21) | copy-start | bytes 49156
where the time goes:
time: 186 us; the launch traced here: 185 us
  Pallas kernels  174 us (94%)
  other arithmetic  6.54 us (4%)
  local copies, waits for them, and re-layouts  4.58 us (2%)
    pallas_call x1, Pallas kernels, summed(): pl.pallas_call(functools.partial(kernel, n_inst, n_rep), out_shape=(jax.S...  174 us
    sub x2, other arithmetic, adamw(): param_new = param - step_rate * (ratio + decay_rate * param)  6.54 us
    unnamed x20, local copies, waits for them, and re-layouts  4.58 us

commit v1 on v0

v1 whole, which is shorter than its diff:
```python
import functools

import jax
import jax.numpy as jnp
from jax import lax
from jax.experimental import pallas as pl
from jax.experimental.pallas import tpu as pltpu
from jax.sharding import PartitionSpec as P

MESH = pl.DeviceIdType.MESH
BUCKETS = 4
BLOCK_ROWS = 256
COLS = 128
SPLIT = 4
LAG = 4
HOP = 4
NEAR = 16
FAR = 32
FRONT = 10
FRONT_TWO = 0
ROUTER_START = 10
VMEM_BYTES = 36 * 2**20


beta_first = 0.9
beta_second = 0.95
step_rate = 0.05
decay_rate = 0.1
epsilon = 1e-08
correct_first = 1.0 - 0.9**10
correct_second = 1.0 - 0.95**10


def adamw(grad, param, moment, second):
    moment_new = beta_first * moment + (1.0 - beta_first) * grad
    second_new = beta_second * second + (1.0 - beta_second) * grad * grad
    ratio = moment_new / correct_first / (jnp.sqrt(second_new / correct_second) + epsilon)
    param_new = param - step_rate * (ratio + decay_rate * param)
    return (param_new, moment_new, second_new)


def both(*terms):
    return functools.reduce(jnp.logical_and, terms)


def whole_part(p):
    return lax.div(p, SPLIT), lax.rem(p, SPLIT)


def is_mixed(chunk, turn):
    last = both(turn == SPLIT - 1, jnp.logical_or(chunk < FRONT, lax.rem(chunk, 2) == 0))
    if FRONT_TWO:
        last = jnp.logical_or(last, both(turn == SPLIT - 2, chunk < FRONT_TWO))
    return last


MIXED_TURNS = (SPLIT - 2, SPLIT - 1) if FRONT_TWO else (SPLIT - 1,)


class Place:
    def __init__(self, n_inst, n_rep):
        self.n_inst, self.n_rep = n_inst, n_rep
        self.bits = n_inst.bit_length() - 1
        self.me, self.rep = lax.axis_index("inst"), lax.axis_index("rep")
        self.left = n_rep // 2 - 1
        low = self.rep <= self.left
        self.depth = jnp.where(low, self.rep, n_rep - 1 - self.rep)
        way = jnp.where(low, 1, -1)
        self.inner, self.outer = self.rep + way, self.rep - way
        self.flips = [(1 - 2 * ((self.me // 2**bit) % 2)) * 2**bit for bit in range(self.bits)]
        self.mixes = n_rep >= 4
        self.mate = jnp.where(self.depth == 0, self.inner, self.outer)
        self.edge = self.depth <= 1
        self.base = 1 + LAG * (self.bits - 1)
        self.top = self.base + HOP * (self.left + 1)
        self.last_step = self.top + HOP * self.left


class Lane:
    def __init__(self, place, kind, dims, refs, sems, finish):
        self.place, self.kind, self.dims = place, kind, dims
        self.parts, self.halves, self.outs, self.ins, self.raws = refs
        self.send, self.recv, self.raw_send, self.raw_recv = sems
        self.finish = finish
        self.stages = len(dims)

    def owner(self, q):
        index = self.place.me
        for at, bit in enumerate(self.dims):
            flip = lax.rem(lax.div(q, 2 ** (self.stages - 1 - at)), 2)
            index = index + flip * self.place.flips[bit]
        return index

    def half_copy(self, stage, p):
        count = self.place.n_inst >> (stage + 1)
        source = self.parts(p) if stage == 0 else self.halves(stage - 1, p)
        return pltpu.make_async_remote_copy(
            src_ref=source.at[pl.ds(count, count)],
            dst_ref=self.halves(stage, p),
            send_sem=self.send.at[stage, p],
            recv_sem=self.recv.at[stage, p],
            device_id={"inst": self.place.me + self.place.flips[self.dims[stage]]},
            device_id_type=MESH,
        )

    def arrive(self, stage, p):
        self.half_copy(stage, p).wait()
        count = self.place.n_inst >> (stage + 1)
        source = self.parts(p) if stage == 0 else self.halves(stage - 1, p)
        into = self.halves(stage, p)
        into[...] += source[pl.ds(0, count)]

    def raw_copy(self, p, at):
        return pltpu.make_async_remote_copy(
            src_ref=self.halves(0, p),
            dst_ref=self.raws(at),
            send_sem=self.raw_send.at[at],
            recv_sem=self.raw_recv.at[at],
            device_id={"rep": self.place.mate},
            device_id_type=MESH,
        )

    def total(self, p):
        return self.halves(self.stages - 1, p)

    def inward(self, p, middle):
        return pltpu.make_async_remote_copy(
            src_ref=self.total(p),
            dst_ref=self.ins(p) if middle else self.outs(p),
            send_sem=self.send.at[self.stages, p],
            recv_sem=self.recv.at[self.stages + 1 if middle else self.stages, p],
            device_id={"rep": self.place.inner},
            device_id_type=MESH,
        )

    def outward(self, p):
        return pltpu.make_async_remote_copy(
            src_ref=self.ins(p),
            dst_ref=self.ins(p),
            send_sem=self.send.at[self.stages + 1, p],
            recv_sem=self.recv.at[self.stages + 1, p],
            device_id={"rep": self.place.outer},
            device_id_type=MESH,
        )


def advance(place, lanes, t, count, mixes):
    mixes = mixes and place.mixes

    def due(lag, body):
        p = t - lag

        @pl.when(both(p >= 0, p < count))
        def _():
            body(p)

    def odd(lane, chunk, turn):
        return lax.rem(chunk + turn + lane.kind + place.depth, 2) == 1

    def each_lane(body):
        for lane in lanes:
            body(lane)

    def raw_at(chunk, turn):
        return chunk if turn == SPLIT - 1 else count // SPLIT + chunk

    def mixed(p, body):
        chunk, turn = whole_part(p)
        for fixed in MIXED_TURNS:

            @pl.when(both(turn == fixed, is_mixed(chunk, fixed)))
            def _():
                for lane in lanes:
                    takes = odd(lane, chunk, fixed)
                    body(lane, chunk, fixed, takes)

    def early(p, body):
        chunk, turn = whole_part(p)

        @pl.when(turn == 0)
        def _():
            for fixed in MIXED_TURNS:

                @pl.when(is_mixed(chunk, fixed))
                def _():
                    for lane in lanes:
                        body(lane, p + fixed, chunk, fixed)

    def plain(p, body):
        if not mixes:
            each_lane(body)
            return
        chunk, turn = whole_part(p)

        @pl.when(jnp.logical_not(is_mixed(chunk, turn)))
        def _():
            each_lane(body)

    def start(p):
        plain(p, lambda lane: lane.half_copy(0, p).start())
        if mixes:
            early(p, lambda lane, at, chunk, turn: lane.half_copy(0, at).start())

    due(0, start)

    def onward(lane, p):
        if place.bits > 1:
            lane.half_copy(1, p).start()

    def first(p):
        def usual(lane):
            lane.arrive(0, p)
            onward(lane, p)

        plain(p, usual)
        if not mixes:
            return

        def taken(lane, chunk, turn, takes):
            at = raw_at(chunk, turn)

            @pl.when(both(place.edge, takes))
            def _():
                lane.raw_copy(p, at).wait_recv()
                into = lane.halves(0, p)
                into[...] += lane.raws(at)[...]

            @pl.when(jnp.logical_or(jnp.logical_not(place.edge), takes))
            def _():
                onward(lane, p)

        mixed(p, taken)

        def given(lane, p, chunk, turn):
            lane.arrive(0, p)

            @pl.when(both(place.edge, jnp.logical_not(odd(lane, chunk, turn))))
            def _():
                lane.raw_copy(p, raw_at(chunk, turn)).start()

        early(p, given)

    due(1, first)

    def later(stage):
        def usual(lane, p):
            lane.arrive(stage, p)
            if stage < place.bits - 1:
                lane.half_copy(stage + 1, p).start()
            else:

                @pl.when(place.depth == 0)
                def _():
                    lane.inward(p, place.left == 0).start()

        def body(p):
            plain(p, lambda lane: usual(lane, p))
            if not mixes:
                return

            def special(lane, chunk, turn, takes):
                gives = both(place.edge, jnp.logical_not(takes))

                @pl.when(jnp.logical_not(gives))
                def _():
                    usual(lane, p)

                if stage == 1:

                    @pl.when(gives)
                    def _():
                        lane.raw_copy(p, raw_at(chunk, turn)).wait_send()

            mixed(p, special)

        return body

    for stage in range(1, place.bits):
        due(1 + LAG * stage, later(stage))

    def collect(p):
        def go(lane):
            if place.left == 1:
                lane.inward(p, True).start()
            else:
                for middle in (False, True):

                    @pl.when((place.depth == place.left) == middle)
                    def _():
                        lane.inward(p, middle).start()

        def usual(lane):
            lane.inward(p, False).wait_recv()
            into = lane.total(p)
            into[...] += lane.outs(p)[...]
            go(lane)

        def special(lane, chunk, turn, takes):
            near = place.depth == 1

            @pl.when(both(near, jnp.logical_not(takes)))
            def _():
                lane.inward(p, False).wait_recv()
                lane.total(p)[...] = lane.outs(p)[...]

            @pl.when(jnp.logical_not(near))
            def _():
                lane.inward(p, False).wait_recv()
                into = lane.total(p)
                into[...] += lane.outs(p)[...]

            go(lane)

        @pl.when(place.depth > 0)
        def _():
            plain(p, usual)
            if mixes:
                mixed(p, special)

    if place.left > 0:
        due(place.base + HOP * place.depth, collect)

    def share(p):
        for lane in lanes:
            lane.outward(p).wait_recv()

            @pl.when(place.depth == place.left)
            def _(lane=lane):
                into = lane.ins(p)
                into[...] += lane.total(p)[...]

            @pl.when(place.depth > 0)
            def _(lane=lane):
                lane.outward(p).start()

        for lane in lanes:
            lane.finish(p)

    due(place.top + HOP * (place.left - place.depth), share)

    def settle(p):
        def sent(lane):
            lane.inward(p, False).wait_send()

        plain(p, sent)
        if mixes:

            def special(lane, chunk, turn, takes):
                @pl.when(jnp.logical_or(place.depth > 0, takes))
                def _():
                    sent(lane)

            mixed(p, special)

        @pl.when(place.depth > 0)
        def _():
            for lane in lanes:
                lane.outward(p).wait_send()

    due(place.last_step, settle)


def kernel(n_inst, n_rep, *refs):
    order_in, acts, keys_in, values_in, logits_in = refs[:5]
    state_in, state = refs[5:11], refs[11:17]
    order, slabs, keys, values, logits, turned, router_all, parts, router_parts = refs[17:26]
    raws, load = refs[26:28]
    scratch = refs[28:]
    place = Place(n_inst, n_rep)
    bits, rep = place.bits, place.rep
    rows = slabs.shape[-1]
    width = router_parts.shape[-1]
    per_bucket = order.shape[0] // BUCKETS
    column_blocks = acts.shape[1] // BLOCK_ROWS
    chunks = keys.shape[1] // COLS
    every = chunks * BUCKETS // 2
    count = every * SPLIT
    size = COLS // SPLIT
    halves = scratch[:bits]
    router_halves = scratch[bits : 2 * bits]
    outs, ins, router_outs, router_ins = scratch[2 * bits : 2 * bits + 4]
    sends, recvs, router_sends, router_recvs, raw_sends, raw_recvs = scratch[2 * bits + 4 :]

    def finish(kind):
        def body(p):
            chunk, turn = whole_part(p)

            @pl.when(turn == SPLIT - 1)
            def _():
                bucket = 2 * lax.div(chunk, chunks) + kind
                start = pl.multiple_of(lax.rem(chunk, chunks) * COLS, COLS)
                slot = lax.rem(chunk * SPLIT, ins.shape[1])
                grad = ins[kind, pl.ds(slot, SPLIT), 0].reshape(COLS, rows).T
                at = (bucket, slice(None), pl.ds(start, COLS))
                fresh = adamw(grad, *[part[at] for part in state[:3]])
                for part, value in zip(state[:3], fresh):
                    part[at] = value

        return body

    def router_finish(p):
        line = state[3].shape[1]
        for at in range(state[3].shape[0]):
            one = (pl.ds(at, 1), slice(None))
            grad = router_ins[0, :, pl.ds(at * line, line)]
            fresh = adamw(grad, *[part[one] for part in state[3:]])
            for part, value in zip(state[3:], fresh):
                part[one] = value

    forward = [0] + list(range(1, bits))
    backward = [0] + list(range(bits - 1, 0, -1))
    lanes = []
    for kind, dims in enumerate((forward, backward)):
        lanes.append(
            Lane(
                place,
                kind,
                dims,
                (
                    lambda p, kind=kind: parts.at[kind, lax.rem(p, 2 * SPLIT)],
                    lambda stage, p, kind=kind: halves[stage].at[
                        kind, lax.rem(p, halves[stage].shape[1])
                    ],
                    lambda p, kind=kind: outs.at[kind, lax.rem(p, outs.shape[1])],
                    lambda p, kind=kind: ins.at[kind, lax.rem(p, ins.shape[1])],
                    lambda at: raws.at[at],
                ),
                (sends.at[kind], recvs.at[kind], raw_sends, raw_recvs),
                finish(kind),
            )
        )
    router = Lane(
        place,
        0,
        forward,
        (
            lambda p: router_parts,
            lambda stage, p: router_halves[stage],
            lambda p: router_outs,
            lambda p: router_ins,
            None,
        ),
        (router_sends, router_recvs, None, None),
        router_finish,
    )

    loads = [
        pltpu.make_async_copy(src, dst, load.at[at])
        for at, (src, dst) in enumerate(
            ((order_in, order), (keys_in, keys), (values_in, values), (logits_in, logits))
        )
    ]
    loads += [
        pltpu.make_async_copy(acts.at[:, pl.ds(at * rows, rows)], slabs.at[at], load.at[4 + at])
        for at in range(slabs.shape[0])
    ]
    states = [
        pltpu.make_async_copy(src, dst, load.at[4 + slabs.shape[0] + at])
        for at, (src, dst) in enumerate(zip(state_in, state))
    ]
    for copy in loads:
        copy.start()

    barrier = pltpu.get_barrier_semaphore()
    for flip in place.flips:
        pl.semaphore_signal(
            barrier, inc=1, device_id={"inst": place.me + flip}, device_id_type=MESH
        )

    @pl.when(rep > 0)
    def _():
        pl.semaphore_signal(barrier, inc=1, device_id={"rep": rep - 1}, device_id_type=MESH)

    @pl.when(rep < n_rep - 1)
    def _():
        pl.semaphore_signal(barrier, inc=1, device_id={"rep": rep + 1}, device_id_type=MESH)

    for copy in loads:
        copy.wait()
    for copy in states:
        copy.start()

    each = n_inst // SPLIT

    def products(chunk, turn):
        column = pl.multiple_of(lax.rem(chunk, chunks) * COLS, COLS)

        @pl.when(turn == 0)
        def _():
            turned[0] = keys[:, pl.ds(column, COLS)].T
            turned[1] = values[:, pl.ds(column, COLS)].T

        slot = lax.rem(chunk, 2) * SPLIT
        for kind, lane in enumerate(lanes):
            bucket = 2 * lax.div(chunk, chunks) + kind
            for i in range(each):
                q = turn * each + i
                first = lane.owner(q) * rows
                block = order[bucket * per_bucket + lax.div(first, BLOCK_ROWS)]
                at = lax.rem(block, column_blocks) * (BLOCK_ROWS // rows)
                at = at + lax.div(lax.rem(first, BLOCK_ROWS), rows)
                full = jnp.dot(
                    turned[lax.div(block, column_blocks)],
                    slabs[at],
                    preferred_element_type=jnp.float32,
                )
                for part in range(SPLIT):
                    parts[kind, slot + part, q] = full[part * size : (part + 1) * size]

    def router_products():
        for at in range(slabs.shape[0]):
            router_all[:, pl.ds(at * rows, rows)] = jnp.dot(
                logits[...], slabs[at], preferred_element_type=jnp.float32
            )
        for q in range(n_inst):
            first = router.owner(q) * width
            router_parts[q] = router_all[
                pl.ds(first // acts.shape[1], 1),
                pl.ds(pl.multiple_of(first % acts.shape[1], width), width),
            ]

    def head(turn, carry):
        products(0, turn)
        return carry

    lax.fori_loop(0, SPLIT, head, 0)
    peers = bits + jnp.where(rep > 0, 1, 0) + jnp.where(rep < n_rep - 1, 1, 0)
    pl.semaphore_wait(barrier, peers)

    def step(t, carry):
        advance(place, lanes, t, count, True)

        @pl.when(t == ROUTER_START)
        def _():
            router_products()
            for copy in states:
                copy.wait()

        @pl.when(both(t >= ROUTER_START, t <= ROUTER_START + place.last_step))
        def _():
            advance(place, [router], t - ROUTER_START, 1, False)

        @pl.when(t < count - SPLIT)
        def _():
            products(lax.div(t, SPLIT) + 1, lax.rem(t, SPLIT))

        return carry

    lax.fori_loop(0, count + place.last_step, step, 0)


def summed(order, acts, keys, values, logits, states, n_inst, n_rep):
    bits = n_inst.bit_length() - 1
    rows = states[0].shape[1]
    width = states[3].size
    kv = keys.shape[1]
    size = COLS // SPLIT
    every = kv // COLS * BUCKETS // 2
    count = every * SPLIT
    vmem = pl.BlockSpec(memory_space=pltpu.VMEM)
    f32 = jnp.float32
    scratch = [
        pltpu.SMEM(order.shape, order.dtype),
        pltpu.VMEM((acts.shape[1] // rows, acts.shape[0], rows), acts.dtype),
        pltpu.VMEM(keys.shape, keys.dtype),
        pltpu.VMEM(values.shape, values.dtype),
        pltpu.VMEM(logits.shape, logits.dtype),
        pltpu.VMEM((2, COLS, acts.shape[0]), acts.dtype),
        pltpu.VMEM((logits.shape[0], acts.shape[1]), f32),
        pltpu.VMEM((2, 2 * SPLIT, n_inst, size, rows), f32),
        pltpu.VMEM((n_inst, 1, width), f32),
        pltpu.VMEM((every + FRONT_TWO, n_inst // 2, size, rows), f32),
        pltpu.SemaphoreType.DMA((acts.shape[1] // rows + 4 + len(states),)),
    ]
    scratch += [
        pltpu.VMEM((2, min(count, FAR if s else NEAR), n_inst >> (s + 1), size, rows), f32)
        for s in range(bits)
    ]
    scratch += [pltpu.VMEM((n_inst >> (s + 1), 1, width), f32) for s in range(bits)]
    scratch += [pltpu.VMEM((2, min(count, FAR), 1, size, rows), f32)] * 2
    scratch += [pltpu.VMEM((1, 1, width), f32)] * 2
    scratch += [pltpu.SemaphoreType.DMA((2, bits + 2, count))] * 2
    scratch += [pltpu.SemaphoreType.DMA((bits + 2, 1))] * 2
    scratch += [pltpu.SemaphoreType.DMA((every + FRONT_TWO,))] * 2
    operands = (order, acts, keys, values, logits, *states)
    return pl.pallas_call(
        functools.partial(kernel, n_inst, n_rep),
        out_shape=tuple(jax.ShapeDtypeStruct(s.shape, s.dtype) for s in states),
        in_specs=[pl.BlockSpec(memory_space=pltpu.HBM)] * len(operands),
        out_specs=(vmem,) * len(states),
        scratch_shapes=scratch,
        compiler_params=pltpu.CompilerParams(
            collective_id=0, has_side_effects=True, vmem_limit_bytes=VMEM_BYTES
        ),
        cost_estimate=pl.CostEstimate(
            flops=4 * acts.shape[0] * acts.shape[1] * kv,
            bytes_accessed=24 * 2**20,
            transcendentals=0,
        ),
    )(*[pltpu.with_memory_space_constraint(x, pltpu.HBM) for x in operands])


def write_kernel(*refs):
    many = (len(refs) - 1) // 2
    copies = [
        pltpu.make_async_copy(refs[at], refs[many + at], refs[-1].at[at]) for at in range(many)
    ]
    for copy in copies:
        copy.start()
    for copy in copies:
        copy.wait()


def written(arrays):
    return pl.pallas_call(
        write_kernel,
        out_shape=tuple(jax.ShapeDtypeStruct(a.shape, a.dtype) for a in arrays),
        in_specs=[pl.BlockSpec(memory_space=pl.ANY)] * len(arrays),
        out_specs=(pl.BlockSpec(memory_space=pltpu.HBM),) * len(arrays),
        scratch_shapes=[pltpu.SemaphoreType.DMA((len(arrays),))],
        compiler_params=pltpu.CompilerParams(vmem_limit_bytes=2**20),
        cost_estimate=pl.CostEstimate(flops=2**20, bytes_accessed=24 * 2**20, transcendentals=0),
    )(*arrays)


def on_device(n_inst, n_rep, acts, grad_keys, grad_values, grad_logits, order, *states):
    fresh = summed(order, acts, grad_keys, grad_values, grad_logits, states, n_inst, n_rep)
    return written(fresh)


def solution(mesh):
    return jax.shard_map(
        functools.partial(on_device, mesh.shape["inst"], mesh.shape["rep"]),
        mesh=mesh,
        in_specs=(
            P(("rep", "inst"), None),
            P(("rep", "inst"), None),
            P(("rep", "inst"), None),
            P(None, ("rep", "inst")),
            P(),
            P(None, "inst", None),
            P(None, "inst", None),
            P(None, "inst", None),
            P("inst", None),
            P("inst", None),
            P("inst", None),
        ),
        out_specs=(
            P(None, "inst", None),
            P(None, "inst", None),
            P(None, "inst", None),
            P("inst", None),
            P("inst", None),
            P("inst", None),
        ),
        check_vma=False,
    )
```

time: 186 us -> 172 us (0.925)
  other arithmetic: 6.54 us -> 0 us
  local copies, waits for them, and re-layouts: 4.58 us -> 0 us
  Pallas kernels: 174 us -> 171 us
    sub x2 -> x0, other arithmetic: 6.54 us -> none  [adamw(): param_new = param - step_rate * (ratio + decay_rate * param)]
    unnamed x20 -> x0, local copies, waits for them, and re-layouts: 4.58 us -> none
    pallas_call x1 -> x2, Pallas kernels: 174 us -> 171 us  [the longest x1 166 us: summed(): pl.pallas_call(functools.partial(kernel, n_inst, n_rep), out_shape=tuple(...]
where the time goes in v1:
time: 172 us
  Pallas kernels  171 us (99%)
    pallas_call x1, Pallas kernels, summed(): pl.pallas_call(functools.partial(kernel, n_inst, n_rep), out_shape=tuple(...  166 us
    pallas_call x1, Pallas kernels, written(): pl.pallas_call(write_kernel, out_shape=tuple((jax.ShapeDtypeStruct(a.shap...  4.72 us

profile of v1, /device:TPU:0, one launch (start us, length us, event | category | flops | bytes accessed | tf_op | source)
XLA Modules:
  0.0 171.7 jit_solution(5840191095445754722)
XLA Ops:
  0.6 166.3 %shard_map.154 = (f32[4,256,1024]{2,1,0:T(8,128)S(1)}, f32[4,256,1024]{2,1,0:T(8,128)S(1)}, f32[4,256,1024]{2,1,0:T(8,128)S(1)}, f32[4,1024]{1,0:T(4,128)S(1)}, ...) custom-call(s32[32]{0:T(128)} %refs_0_.1, bf16[1024,4096]{1,0:T(8,128)(2,1)} %refs_1_.1, bf16[1024,1024]{1,0:T(8,128)(2,1)} %refs_2_.1, ...), custom_call_target="tpu_custom_call" | custom-call | flops 17179869184 | bytes 25165824 | tf_op jit(solution)/shard_map/pallas_call | solution.py:586
  167.0 4.7 %shard_map.155 = (f32[4,256,1024]{2,1,0:T(8,128)}, f32[4,256,1024]{2,1,0:T(8,128)}, f32[4,256,1024]{2,1,0:T(8,128)}, f32[4,1024]{1,0:T(4,128)}, f32[4,1024]{1,0:T(4,128)}, /*index=5*/f32[4,1024]{1,0:T(4,128)}) custom-call(f32[4,256,1024]{2,1,0:T(8,128)S(1)} %get-tuple-element.12.refs_0_, f32[4,256,1024]{2,1,0:T(8,128)S(1)} %get-tuple-element.13.refs_1_, ...), custom_call_target="tpu_custom_call" | custom-call | flops 1048576 | bytes 25165824 | tf_op jit(solution)/shard_map/pallas_call | solution.py:615

commit v2 on v1

--- a/solution.py
+++ b/solution.py
@@ -16,6 +16,7 @@
 HOP = 4
 NEAR = 16
 FAR = 32
+SIGNALS = 16
 FRONT = 10
 FRONT_TWO = 0
 ROUTER_START = 10
@@ -77,12 +78,13 @@
 
 
 class Lane:
-    def __init__(self, place, kind, dims, refs, sems, finish):
+    def __init__(self, place, kind, dims, refs, sems, signals, finish):
         self.place, self.kind, self.dims = place, kind, dims
         self.parts, self.halves, self.outs, self.ins, self.raws = refs
         self.send, self.recv, self.raw_send, self.raw_recv = sems
         self.finish = finish
         self.stages = len(dims)
+        self.signals = signals
 
     def owner(self, q):
         index = self.place.me
@@ -97,8 +99,8 @@
         return pltpu.make_async_remote_copy(
             src_ref=source.at[pl.ds(count, count)],
             dst_ref=self.halves(stage, p),
-            send_sem=self.send.at[stage, p],
-            recv_sem=self.recv.at[stage, p],
+            send_sem=self.send.at[stage, lax.rem(p, self.signals)],
+            recv_sem=self.recv.at[stage, lax.rem(p, self.signals)],
             device_id={"inst": self.place.me + self.place.flips[self.dims[stage]]},
             device_id_type=MESH,
         )
@@ -127,8 +129,10 @@
         return pltpu.make_async_remote_copy(
             src_ref=self.total(p),
             dst_ref=self.ins(p) if middle else self.outs(p),
-            send_sem=self.send.at[self.stages, p],
-            recv_sem=self.recv.at[self.stages + 1 if middle else self.stages, p],
+            send_sem=self.send.at[self.stages, lax.rem(p, self.signals)],
+            recv_sem=self.recv.at[
+                self.stages + 1 if middle else self.stages, lax.rem(p, self.signals)
+            ],
             device_id={"rep": self.place.inner},
             device_id_type=MESH,
         )
@@ -137,14 +141,18 @@
         return pltpu.make_async_remote_copy(
             src_ref=self.ins(p),
             dst_ref=self.ins(p),
-            send_sem=self.send.at[self.stages + 1, p],
-            recv_sem=self.recv.at[self.stages + 1, p],
+            send_sem=self.send.at[self.stages + 1, lax.rem(p, self.signals)],
+            recv_sem=self.recv.at[self.stages + 1, lax.rem(p, self.signals)],
             device_id={"rep": self.place.outer},
             device_id_type=MESH,
         )
 
 
-def advance(place, lanes, t, count, mixes):
+def begin(place, lanes, p, mixes):
+    advance(place, lanes, jnp.int32(p), p + 1, mixes, only_start=True)
+
+
+def advance(place, lanes, t, count, mixes, least=0, only_start=False):
     mixes = mixes and place.mixes
 
     def due(lag, body):
@@ -201,7 +209,13 @@
         if mixes:
             early(p, lambda lane, at, chunk, turn: lane.half_copy(0, at).start())
 
-    due(0, start)
+    if only_start:
+        start(t)
+        return
+
+    @pl.when(both(t >= least, t < count))
+    def _():
+        start(t)
 
     def onward(lane, p):
         if place.bits > 1:
@@ -426,6 +440,7 @@
                     lambda at: raws.at[at],
                 ),
                 (sends.at[kind], recvs.at[kind], raw_sends, raw_recvs),
+                SIGNALS,
                 finish(kind),
             )
         )
@@ -441,24 +456,24 @@
             None,
         ),
         (router_sends, router_recvs, None, None),
+        1,
         router_finish,
     )
 
+    lead, rest = pl.ds(0, COLS), pl.ds(COLS, keys.shape[1] - COLS)
+    early = [(order_in, order)]
+    early += [(keys_in.at[:, lead], keys.at[:, lead]), (values_in.at[:, lead], values.at[:, lead])]
+    early += [
+        (acts.at[:, pl.ds(at * rows, rows)], slabs.at[at]) for at in range(slabs.shape[0])
+    ]
+    late = [(keys_in.at[:, rest], keys.at[:, rest]), (values_in.at[:, rest], values.at[:, rest])]
+    late += [(logits_in, logits)]
+    late += list(zip(state_in, state))
     loads = [
-        pltpu.make_async_copy(src, dst, load.at[at])
-        for at, (src, dst) in enumerate(
-            ((order_in, order), (keys_in, keys), (values_in, values), (logits_in, logits))
-        )
+        pltpu.make_async_copy(src, dst, load.at[at]) for at, (src, dst) in enumerate(early + late)
     ]
-    loads += [
-        pltpu.make_async_copy(acts.at[:, pl.ds(at * rows, rows)], slabs.at[at], load.at[4 + at])
-        for at in range(slabs.shape[0])
-    ]
-    states = [
-        pltpu.make_async_copy(src, dst, load.at[4 + slabs.shape[0] + at])
-        for at, (src, dst) in enumerate(zip(state_in, state))
-    ]
-    for copy in loads:
+    early, late, states = loads[: len(early)], loads[len(early) : -len(state)], loads[-len(state) :]
+    for copy in early + late:
         copy.start()
 
     barrier = pltpu.get_barrier_semaphore()
@@ -475,21 +490,17 @@
     def _():
         pl.semaphore_signal(barrier, inc=1, device_id={"rep": rep + 1}, device_id_type=MESH)
 
-    for copy in loads:
+    for copy in early:
         copy.wait()
-    for copy in states:
-        copy.start()
 
     each = n_inst // SPLIT
 
+    def turn_over(chunk):
+        column = pl.multiple_of(lax.rem(chunk, chunks) * COLS, COLS)
+        turned[0] = keys[:, pl.ds(column, COLS)].T
+        turned[1] = values[:, pl.ds(column, COLS)].T
+
     def products(chunk, turn):
-        column = pl.multiple_of(lax.rem(chunk, chunks) * COLS, COLS)
-
-        @pl.when(turn == 0)
-        def _():
-            turned[0] = keys[:, pl.ds(column, COLS)].T
-            turned[1] = values[:, pl.ds(column, COLS)].T
-
         slot = lax.rem(chunk, 2) * SPLIT
         for kind, lane in enumerate(lanes):
             bucket = 2 * lax.div(chunk, chunks) + kind
@@ -523,12 +534,19 @@
         products(0, turn)
         return carry
 
-    lax.fori_loop(0, SPLIT, head, 0)
+    turn_over(0)
+    lax.fori_loop(SPLIT // 2, SPLIT, head, 0)
     peers = bits + jnp.where(rep > 0, 1, 0) + jnp.where(rep < n_rep - 1, 1, 0)
     pl.semaphore_wait(barrier, peers)
+    begin(place, lanes, 0, True)
+    lax.fori_loop(0, SPLIT // 2, head, 0)
+    for copy in states:
+        copy.start()
+    for copy in late:
+        copy.wait()
 
     def step(t, carry):
-        advance(place, lanes, t, count, True)
+        advance(place, lanes, t, count, True, least=1)
 
         @pl.when(t == ROUTER_START)
         def _():
@@ -542,7 +560,13 @@
 
         @pl.when(t < count - SPLIT)
         def _():
-            products(lax.div(t, SPLIT) + 1, lax.rem(t, SPLIT))
+            chunk, turn = lax.div(t, SPLIT) + 1, lax.rem(t, SPLIT)
+
+            @pl.when(turn == 0)
+            def _():
+                turn_over(chunk)
+
+            products(chunk, turn)
 
         return carry
 
@@ -570,7 +594,7 @@
         pltpu.VMEM((2, 2 * SPLIT, n_inst, size, rows), f32),
         pltpu.VMEM((n_inst, 1, width), f32),
         pltpu.VMEM((every + FRONT_TWO, n_inst // 2, size, rows), f32),
-        pltpu.SemaphoreType.DMA((acts.shape[1] // rows + 4 + len(states),)),
+        pltpu.SemaphoreType.DMA((acts.shape[1] // rows + 6 + len(states),)),
     ]
     scratch += [
         pltpu.VMEM((2, min(count, FAR if s else NEAR), n_inst >> (s + 1), size, rows), f32)
@@ -579,7 +603,7 @@
     scratch += [pltpu.VMEM((n_inst >> (s + 1), 1, width), f32) for s in range(bits)]
     scratch += [pltpu.VMEM((2, min(count, FAR), 1, size, rows), f32)] * 2
     scratch += [pltpu.VMEM((1, 1, width), f32)] * 2
-    scratch += [pltpu.SemaphoreType.DMA((2, bits + 2, count))] * 2
+    scratch += [pltpu.SemaphoreType.DMA((2, bits + 2, SIGNALS))] * 2
     scratch += [pltpu.SemaphoreType.DMA((bits + 2, 1))] * 2
     scratch += [pltpu.SemaphoreType.DMA((every + FRONT_TWO,))] * 2
     operands = (order, acts, keys, values, logits, *states)

time: 172 us -> 161 us (0.936)
  Pallas kernels: 171 us -> 160 us
    pallas_call x1, Pallas kernels: 166 us -> 156 us  [summed(): pl.pallas_call(functools.partial(kernel, n_inst, n_rep), out_shape=tuple(...]
where the time goes in v2:
time: 161 us
  Pallas kernels  160 us (99%)
    pallas_call x1, Pallas kernels, summed(): pl.pallas_call(functools.partial(kernel, n_inst, n_rep), out_shape=tuple(...  156 us
    pallas_call x1, Pallas kernels, written(): pl.pallas_call(write_kernel, out_shape=tuple((jax.ShapeDtypeStruct(a.shap...  4.72 us

profile of v2, /device:TPU:0, one launch (start us, length us, event | category | flops | bytes accessed | tf_op | source)
XLA Modules:
  0.0 160.9 jit_solution(9394566678833538736)
XLA Ops:
  0.6 155.5 %shard_map.154 = (f32[4,256,1024]{2,1,0:T(8,128)S(1)}, f32[4,256,1024]{2,1,0:T(8,128)S(1)}, f32[4,256,1024]{2,1,0:T(8,128)S(1)}, f32[4,1024]{1,0:T(4,128)S(1)}, ...) custom-call(s32[32]{0:T(128)} %refs_0_.1, bf16[1024,4096]{1,0:T(8,128)(2,1)} %refs_1_.1, bf16[1024,1024]{1,0:T(8,128)(2,1)} %refs_2_.1, ...), custom_call_target="tpu_custom_call" | custom-call | flops 17179869184 | bytes 25165824 | tf_op jit(solution)/shard_map/pallas_call | solution.py:610
  156.2 4.7 %shard_map.155 = (f32[4,256,1024]{2,1,0:T(8,128)}, f32[4,256,1024]{2,1,0:T(8,128)}, f32[4,256,1024]{2,1,0:T(8,128)}, f32[4,1024]{1,0:T(4,128)}, f32[4,1024]{1,0:T(4,128)}, /*index=5*/f32[4,1024]{1,0:T(4,128)}) custom-call(f32[4,256,1024]{2,1,0:T(8,128)S(1)} %get-tuple-element.12.refs_0_, f32[4,256,1024]{2,1,0:T(8,128)S(1)} %get-tuple-element.13.refs_1_, ...), custom_call_target="tpu_custom_call" | custom-call | flops 1048576 | bytes 25165824 | tf_op jit(solution)/shard_map/pallas_call | solution.py:639

commit v3 on v2

--- a/solution.py
+++ b/solution.py
@@ -12,13 +12,15 @@
 BLOCK_ROWS = 256
 COLS = 128
 SPLIT = 4
-LAG = 4
-HOP = 4
+LAG = 3
+HOP = 3
 NEAR = 16
 FAR = 32
-SIGNALS = 16
-FRONT = 10
-FRONT_TWO = 0
+SIGNALS = 12
+ENDS = 14
+BACK = 2
+MIDDLE = 12
+RAW = 4
 ROUTER_START = 10
 VMEM_BYTES = 36 * 2**20
 
@@ -48,14 +50,21 @@
     return lax.div(p, SPLIT), lax.rem(p, SPLIT)
 
 
+def in_ends(chunk):
+    return chunk < ENDS
+
+
+def in_middle(chunk):
+    return jnp.logical_or(chunk < 4, both(lax.rem(chunk, 2) == 1, chunk < MIDDLE))
+
+
 def is_mixed(chunk, turn):
-    last = both(turn == SPLIT - 1, jnp.logical_or(chunk < FRONT, lax.rem(chunk, 2) == 0))
-    if FRONT_TWO:
-        last = jnp.logical_or(last, both(turn == SPLIT - 2, chunk < FRONT_TWO))
-    return last
-
-
-MIXED_TURNS = (SPLIT - 2, SPLIT - 1) if FRONT_TWO else (SPLIT - 1,)
+    return jnp.logical_or(
+        both(turn == SPLIT - 1, in_ends(chunk)), both(turn == SPLIT - 2, in_middle(chunk))
+    )
+
+
+MIXED_TURNS = (SPLIT - 1, SPLIT - 2)
 
 
 class Place:
@@ -71,7 +80,7 @@
         self.flips = [(1 - 2 * ((self.me // 2**bit) % 2)) * 2**bit for bit in range(self.bits)]
         self.mixes = n_rep >= 4
         self.mate = jnp.where(self.depth == 0, self.inner, self.outer)
-        self.edge = self.depth <= 1
+        self.side = jnp.where(low, 0, 1)
         self.base = 1 + LAG * (self.bits - 1)
         self.top = self.base + HOP * (self.left + 1)
         self.last_step = self.top + HOP * self.left
@@ -112,13 +121,27 @@
         into = self.halves(stage, p)
         into[...] += source[pl.ds(0, count)]
 
-    def raw_copy(self, p, at):
+    def role(self, chunk, turn):
+        depth = self.place.depth
+        if turn == SPLIT - 1:
+            inward = lax.rem(chunk + self.kind, 2) == 0
+            outward = both(jnp.logical_not(inward), lax.rem(lax.div(chunk, 2), BACK) == 0)
+            end, near = depth == 0, depth == 1
+            gives = jnp.logical_or(both(inward, end), both(outward, near))
+            takes = jnp.logical_or(both(inward, near), both(outward, end))
+            return gives, takes, both(inward, near)
+        middle = depth == self.place.left
+        even = lax.rem(chunk + self.kind + self.place.side, 2) == 0
+        return both(middle, even), both(middle, jnp.logical_not(even)), depth < 0
+
+    def raw_copy(self, p, chunk, turn):
+        at = lax.rem(chunk, RAW) + (RAW if turn == SPLIT - 2 else 0)
         return pltpu.make_async_remote_copy(
             src_ref=self.halves(0, p),
             dst_ref=self.raws(at),
             send_sem=self.raw_send.at[at],
             recv_sem=self.raw_recv.at[at],
-            device_id={"rep": self.place.mate},
+            device_id={"rep": self.place.mate if turn == SPLIT - 1 else self.place.inner},
             device_id_type=MESH,
         )
 
@@ -162,16 +185,10 @@
         def _():
             body(p)
 
-    def odd(lane, chunk, turn):
-        return lax.rem(chunk + turn + lane.kind + place.depth, 2) == 1
-
     def each_lane(body):
         for lane in lanes:
             body(lane)
 
-    def raw_at(chunk, turn):
-        return chunk if turn == SPLIT - 1 else count // SPLIT + chunk
-
     def mixed(p, body):
         chunk, turn = whole_part(p)
         for fixed in MIXED_TURNS:
@@ -179,8 +196,20 @@
             @pl.when(both(turn == fixed, is_mixed(chunk, fixed)))
             def _():
                 for lane in lanes:
-                    takes = odd(lane, chunk, fixed)
-                    body(lane, chunk, fixed, takes)
+                    body(lane, p, chunk, fixed, *lane.role(chunk, fixed))
+
+    def together(p, body):
+        chunk, turn = whole_part(p)
+
+        @pl.when(turn == SPLIT - 1)
+        def _():
+            for fixed in MIXED_TURNS:
+
+                @pl.when(is_mixed(chunk, fixed))
+                def _():
+                    for lane in lanes:
+                        at = p + fixed - SPLIT + 1
+                        body(lane, at, chunk, fixed, *lane.role(chunk, fixed))
 
     def early(p, body):
         chunk, turn = whole_part(p)
@@ -230,27 +259,25 @@
         if not mixes:
             return
 
-        def taken(lane, chunk, turn, takes):
-            at = raw_at(chunk, turn)
-
-            @pl.when(both(place.edge, takes))
+        def taken(lane, p, chunk, turn, gives, takes, misses):
+            @pl.when(takes)
             def _():
-                lane.raw_copy(p, at).wait_recv()
+                lane.raw_copy(p, chunk, turn).wait_recv()
                 into = lane.halves(0, p)
-                into[...] += lane.raws(at)[...]
-
-            @pl.when(jnp.logical_or(jnp.logical_not(place.edge), takes))
+                into[...] += lane.raws(lax.rem(chunk, RAW) + (RAW if turn == SPLIT - 2 else 0))[...]
+
+            @pl.when(jnp.logical_not(gives))
             def _():
                 onward(lane, p)
 
-        mixed(p, taken)
+        together(p, taken)
 
         def given(lane, p, chunk, turn):
             lane.arrive(0, p)
 
-            @pl.when(both(place.edge, jnp.logical_not(odd(lane, chunk, turn))))
+            @pl.when(lane.role(chunk, turn)[0])
             def _():
-                lane.raw_copy(p, raw_at(chunk, turn)).start()
+                lane.raw_copy(p, chunk, turn).start()
 
         early(p, given)
 
@@ -272,9 +299,7 @@
             if not mixes:
                 return
 
-            def special(lane, chunk, turn, takes):
-                gives = both(place.edge, jnp.logical_not(takes))
-
+            def special(lane, p, chunk, turn, gives, takes, misses):
                 @pl.when(jnp.logical_not(gives))
                 def _():
                     usual(lane, p)
@@ -283,7 +308,7 @@
 
                     @pl.when(gives)
                     def _():
-                        lane.raw_copy(p, raw_at(chunk, turn)).wait_send()
+                        lane.raw_copy(p, chunk, turn).wait_send()
 
             mixed(p, special)
 
@@ -309,15 +334,13 @@
             into[...] += lane.outs(p)[...]
             go(lane)
 
-        def special(lane, chunk, turn, takes):
-            near = place.depth == 1
-
-            @pl.when(both(near, jnp.logical_not(takes)))
+        def special(lane, p, chunk, turn, gives, takes, misses):
+            @pl.when(gives)
             def _():
                 lane.inward(p, False).wait_recv()
                 lane.total(p)[...] = lane.outs(p)[...]
 
-            @pl.when(jnp.logical_not(near))
+            @pl.when(jnp.logical_not(jnp.logical_or(gives, misses)))
             def _():
                 lane.inward(p, False).wait_recv()
                 into = lane.total(p)
@@ -359,8 +382,8 @@
         plain(p, sent)
         if mixes:
 
-            def special(lane, chunk, turn, takes):
-                @pl.when(jnp.logical_or(place.depth > 0, takes))
+            def special(lane, p, chunk, turn, gives, takes, misses):
+                @pl.when(jnp.logical_or(place.depth > 0, jnp.logical_not(gives)))
                 def _():
                     sent(lane)
 
@@ -593,7 +616,7 @@
         pltpu.VMEM((logits.shape[0], acts.shape[1]), f32),
         pltpu.VMEM((2, 2 * SPLIT, n_inst, size, rows), f32),
         pltpu.VMEM((n_inst, 1, width), f32),
-        pltpu.VMEM((every + FRONT_TWO, n_inst // 2, size, rows), f32),
+        pltpu.VMEM((2 * RAW, n_inst // 2, size, rows), f32),
         pltpu.SemaphoreType.DMA((acts.shape[1] // rows + 6 + len(states),)),
     ]
     scratch += [
@@ -605,7 +628,7 @@
     scratch += [pltpu.VMEM((1, 1, width), f32)] * 2
     scratch += [pltpu.SemaphoreType.DMA((2, bits + 2, SIGNALS))] * 2
     scratch += [pltpu.SemaphoreType.DMA((bits + 2, 1))] * 2
-    scratch += [pltpu.SemaphoreType.DMA((every + FRONT_TWO,))] * 2
+    scratch += [pltpu.SemaphoreType.DMA((2 * RAW,))] * 2
     operands = (order, acts, keys, values, logits, *states)
     return pl.pallas_call(
         functools.partial(kernel, n_inst, n_rep),

time: 161 us -> 160 us (level)
  no operation moved by 1% of the time
where the time goes in v3:
time: 160 us
  Pallas kernels  159 us (99%)
    pallas_call x1, Pallas kernels, summed(): pl.pallas_call(functools.partial(kernel, n_inst, n_rep), out_shape=tuple(...  155 us
    pallas_call x1, Pallas kernels, written(): pl.pallas_call(write_kernel, out_shape=tuple((jax.ShapeDtypeStruct(a.shap...  4.72 us

profile of v3, /device:TPU:0, one launch (start us, length us, event | category | flops | bytes accessed | tf_op | source)
XLA Modules:
  0.0 159.9 jit_solution(3897703084906011541)
XLA Ops:
  0.6 154.5 %shard_map.154 = (f32[4,256,1024]{2,1,0:T(8,128)S(1)}, f32[4,256,1024]{2,1,0:T(8,128)S(1)}, f32[4,256,1024]{2,1,0:T(8,128)S(1)}, f32[4,1024]{1,0:T(4,128)S(1)}, ...) custom-call(s32[32]{0:T(128)} %refs_0_.1, bf16[1024,4096]{1,0:T(8,128)(2,1)} %refs_1_.1, bf16[1024,1024]{1,0:T(8,128)(2,1)} %refs_2_.1, ...), custom_call_target="tpu_custom_call" | custom-call | flops 17179869184 | bytes 25165824 | tf_op jit(solution)/shard_map/pallas_call | solution.py:633
  155.2 4.7 %shard_map.155 = (f32[4,256,1024]{2,1,0:T(8,128)}, f32[4,256,1024]{2,1,0:T(8,128)}, f32[4,256,1024]{2,1,0:T(8,128)}, f32[4,1024]{1,0:T(4,128)}, f32[4,1024]{1,0:T(4,128)}, /*index=5*/f32[4,1024]{1,0:T(4,128)}) custom-call(f32[4,256,1024]{2,1,0:T(8,128)S(1)} %get-tuple-element.12.refs_0_, f32[4,256,1024]{2,1,0:T(8,128)S(1)} %get-tuple-element.13.refs_1_, ...), custom_call_target="tpu_custom_call" | custom-call | flops 1048576 | bytes 25165824 | tf_op jit(solution)/shard_map/pallas_call | solution.py:662

commit v4 on v3

--- a/solution.py
+++ b/solution.py
@@ -16,7 +16,7 @@
 HOP = 3
 NEAR = 16
 FAR = 32
-SIGNALS = 12
+SIGNALS = 10
 ENDS = 14
 BACK = 2
 MIDDLE = 12

time: 160 us -> 160 us (level)
  no operation moved by 1% of the time
where the time goes in v4:
time: 160 us
  Pallas kernels  159 us (99%)
    pallas_call x1, Pallas kernels, summed(): pl.pallas_call(functools.partial(kernel, n_inst, n_rep), out_shape=tuple(...  154 us
    pallas_call x1, Pallas kernels, written(): pl.pallas_call(write_kernel, out_shape=tuple((jax.ShapeDtypeStruct(a.shap...  4.72 us

profile of v4, /device:TPU:0, one launch (start us, length us, event | category | flops | bytes accessed | tf_op | source)
XLA Modules:
  0.0 159.5 jit_solution(13482961101783155935)
XLA Ops:
  0.6 154.2 %shard_map.154 = (f32[4,256,1024]{2,1,0:T(8,128)S(1)}, f32[4,256,1024]{2,1,0:T(8,128)S(1)}, f32[4,256,1024]{2,1,0:T(8,128)S(1)}, f32[4,1024]{1,0:T(4,128)S(1)}, ...) custom-call(s32[32]{0:T(128)} %refs_0_.1, bf16[1024,4096]{1,0:T(8,128)(2,1)} %refs_1_.1, bf16[1024,1024]{1,0:T(8,128)(2,1)} %refs_2_.1, ...), custom_call_target="tpu_custom_call" | custom-call | flops 17179869184 | bytes 25165824 | tf_op jit(solution)/shard_map/pallas_call | solution.py:633
  154.8 4.7 %shard_map.155 = (f32[4,256,1024]{2,1,0:T(8,128)}, f32[4,256,1024]{2,1,0:T(8,128)}, f32[4,256,1024]{2,1,0:T(8,128)}, f32[4,1024]{1,0:T(4,128)}, f32[4,1024]{1,0:T(4,128)}, /*index=5*/f32[4,1024]{1,0:T(4,128)}) custom-call(f32[4,256,1024]{2,1,0:T(8,128)S(1)} %get-tuple-element.12.refs_0_, f32[4,256,1024]{2,1,0:T(8,128)S(1)} %get-tuple-element.13.refs_1_, ...), custom_call_target="tpu_custom_call" | custom-call | flops 1048576 | bytes 25165824 | tf_op jit(solution)/shard_map/pallas_call | solution.py:662
